TPU v7x, 32 devices: a whole 2x2x4 slice. The times are simulated.
32 devices in a mesh: expert: 8 (over z, x), pair: 4 (over y, core).
Axes of the slice: x: 2, y: 2, z: 4, core: 2. Of those that a mesh axis runs over, the one named last changes fastest.
Arguments:
- tokens: bfloat16 [12288, 2048], P(('expert', 'pair')), may hold values from -6 to 6
- token_ids: int32 [12288], P(('expert', 'pair')), may hold values from 0 to 8191
- table: int32 [8192], replicated, may hold values from 0 to 15
- w_in: bfloat16 [16, 2048, 2048], P('expert', None, 'pair'), may hold values from -0.125 to 0.125
- w_out: bfloat16 [16, 2048, 2048], P('expert', 'pair'), may hold values from -0.125 to 0.125
Outputs:
- mixed: bfloat16 [12288, 2048], P(('expert', 'pair'))
All inputs are finite; a program needn't handle non-finite values.
Results may differ from a plain program's by a relative error of at most 0.0085.
Values may be sent and summed in bfloat16 or wider, within the bound.
A program may use at most 192 MiB of HBM per device.

v0:
```python
import functools

import jax
import jax.numpy as jnp
from jax import lax
from jax.experimental import pallas as pl
from jax.experimental.pallas import tpu as pltpu
from jax.sharding import PartitionSpec as P

ROWS = 16
TILE = 256
LAST_PIECES = 4
LANES = 128
MESH = pl.DeviceIdType.MESH


def exact_dot(a, b):
    return jnp.dot(a, b, preferred_element_type=jnp.float32)


def across(me, j):
    other = me
    bit = 1
    while bit <= j:
        if j & bit:
            other = other + bit * (1 - 2 * (me // bit % 2))
        bit *= 2
    return other


def send_order(chunks, n):
    first = [(c, 1) for c in range(chunks)]
    return first + [(c, j) for c in range(chunks) for j in range(2, n)]


def layer_kernel(
    n,
    packed,
    w_in,
    w_out,
    back,
    first,
    second,
    rows,
    hidden,
    part,
    near,
    far,
    own_sem,
    w_sem,
    go_sem,
    come_sem,
    pair_go,
    pair_come,
    part_go,
    part_come,
    ret_go,
    ret_come,
    ret_own,
):
    chunks = packed.shape[0]
    per_expert = chunks // w_in.shape[0]
    me = lax.axis_index("expert")
    at = lax.axis_index("pair")
    core = {"pair": at + 1 - 2 * (at % 2)}
    chip = {"pair": (at + 2) % 4}
    ahead = [{"expert": across(me, j)} for j in range(n)]

    w_copies = [
        pltpu.make_async_copy(w_in, first, w_sem.at[0]),
        pltpu.make_async_copy(w_out, second, w_sem.at[1]),
    ]
    for copy in w_copies:
        copy.start()

    barrier = pltpu.get_barrier_semaphore()
    for peer in [core, chip] + ahead[1:]:
        pl.semaphore_signal(barrier, inc=1, device_id=peer, device_id_type=MESH)
    pl.semaphore_wait(barrier, n + 1)

    def remote(src, dst, send, recv, peer):
        copy = pltpu.make_async_remote_copy(
            src_ref=src,
            dst_ref=dst,
            send_sem=send,
            recv_sem=recv,
            device_id=peer,
            device_id_type=MESH,
        )
        copy.start()
        return copy

    sent = []
    dispatch = {}
    links = {}

    def pair_send(kind, c, src, dst, peer):
        links[kind, c] = remote(src, dst, pair_go.at[kind, c], pair_come.at[kind, c], peer)

    def blocks(lo, hi):
        return pl.ds(lo * ROWS, (hi - lo) * ROWS)

    def send_block(c, j):
        dispatch[c, j] = remote(
            packed.at[c, blocks(j, j + 1)],
            rows.at[c, 0, blocks(j, j + 1)],
            go_sem.at[c, j],
            come_sem.at[c, j],
            ahead[j],
        )

    for c, j in send_order(chunks, n):
        send_block(c, j)
    own_copies = []
    for c in range(chunks):
        own = blocks(0, 1)
        pair_send(0, c, packed.at[c, own], rows.at[c, 2, own], chip)
        pair_send(1, c, packed.at[c, own], rows.at[c, 1, own], core)
        copy = pltpu.make_async_copy(packed.at[c, own], rows.at[c, 0, own], own_sem.at[c])
        copy.start()
        own_copies.append(copy)

    groups = [(1, 2), (2, n // 2), (n // 2, n)]

    def spread(c, g):
        lo, hi = groups[g]
        for j in range(lo, hi):
            dispatch[c, j].wait_recv()
        some = blocks(lo, hi)
        pair_send(2 + 2 * g, c, rows.at[c, 0, some], rows.at[c, 2, some], chip)
        pair_send(3 + 2 * g, c, rows.at[c, 0, some], rows.at[c, 1, some], core)

    def relay(c):
        for kind in (0, 2, 4, 6):
            links[kind, c].wait_recv()
        pair_send(8, c, rows.at[c, 2], rows.at[c, 3], core)

    def pieces(c):
        return LAST_PIECES if c == chunks - 1 else 1

    def columns(c, q):
        size = part.shape[3] // pieces(c)
        return pl.ds(q * size, size)

    def part_send(kind, c, q, src, dst, peer):
        links[kind, c, q] = remote(
            src, dst, part_go.at[kind, c, q], part_come.at[kind, c, q], peer
        )

    def compute(c):
        e = c // per_expert
        if c == 0:
            for copy in w_copies:
                copy.wait()
        own_copies[c].wait()
        for kind in (1, 3, 5, 7, 8):
            links[kind, c].wait_recv()
        block = rows.shape[2]

        def project_in(t, carry):
            cols = pl.ds(pl.multiple_of(t * TILE, TILE), TILE)
            x = rows[c].reshape(4 * block, rows.shape[3])
            h = exact_dot(x, first[e, :, cols])
            hidden[:, cols] = jnp.maximum(h, 0.0).astype(jnp.bfloat16)
            return carry

        lax.fori_loop(0, first.shape[2] // TILE, project_in, 0)

        def project_out(t, carry):
            cols = pl.ds(pl.multiple_of(t * TILE, TILE), TILE)
            y = exact_dot(hidden[...], second[e, :, cols]).astype(jnp.bfloat16)
            for k in range(4):
                part[c, k, :, cols] = y[k * block : (k + 1) * block]
            return carry

        steps = second.shape[2] // TILE // pieces(c)
        for q in range(pieces(c)):
            lax.fori_loop(q * steps, (q + 1) * steps, project_out, 0)
            cols = columns(c, q)
            part_send(0, c, q, part.at[c, 3, :, cols], near.at[c, 1, :, cols], core)
            part_send(1, c, q, part.at[c, 1, :, cols], near.at[c, 0, :, cols], core)

    def over_rows(body):
        def step(t, carry):
            body(pl.ds(pl.multiple_of(t * ROWS, ROWS), ROWS))
            return carry

        lax.fori_loop(0, n, step, 0)

    def wide(x):
        return x.astype(jnp.float32)

    def cross(c):
        for q in range(pieces(c)):
            links[0, c, q].wait_recv()
            cols = columns(c, q)

            def add(r):
                both = wide(part[c, 2, r, cols]) + wide(near[c, 1, r, cols])
                part[c, 2, r, cols] = both.astype(jnp.bfloat16)

            over_rows(add)
            part_send(2, c, q, part.at[c, 2, :, cols], far.at[c, :, cols], chip)

    def finish(c):
        for q in range(pieces(c)):
            links[1, c, q].wait_recv()
            links[2, c, q].wait_recv()
            cols = columns(c, q)

            def add(r):
                both = wide(part[c, 0, r, cols]) + wide(near[c, 0, r, cols])
                both = both + wide(far[c, r, cols])
                part[c, 0, r, cols] = both.astype(jnp.bfloat16)

            over_rows(add)
            for j in range(1, n):
                some = blocks(j, j + 1)
                sent.append(
                    remote(
                        part.at[c, 0, some, cols],
                        back.at[c, some, cols],
                        ret_go.at[c, q, j],
                        ret_come.at[c, q, j],
                        ahead[j],
                    )
                )
            own = blocks(0, 1)
            copy = pltpu.make_async_copy(
                part.at[c, 0, own, cols], back.at[c, own, cols], ret_own.at[c, q]
            )
            copy.start()
            sent.append(copy)

    def spread0(c):
        spread(c, 1)

    def spread1(c):
        spread(c, 2)

    for c in range(chunks):
        spread(c, 0)

    order = [(spread0, 0), (relay, 1), (spread1, 0), (compute, 1), (cross, 1), (finish, 2)]
    for i in range(chunks + 3):
        for stage, late in order:
            if 0 <= i - late < chunks:
                stage(i - late)

    for copy in dispatch.values():
        copy.wait_send()
    for copy in links.values():
        copy.wait_send()
    for copy in sent:
        copy.wait()


def look_up(table, ids):
    lines = table.reshape(-1, LANES).astype(jnp.bfloat16)
    line = ids[:, None] // LANES == jnp.arange(lines.shape[0], dtype=jnp.int32)[None, :]
    found = exact_dot(line.astype(jnp.bfloat16), lines)
    lane = ids[:, None] % LANES == jnp.arange(LANES, dtype=jnp.int32)[None, :]
    return jnp.sum(jnp.where(lane, found, 0.0), axis=1).astype(jnp.int32)


def expert_layer(packed, w_in, w_out, n):
    chunks, block, width = packed.shape
    quarter = w_in.shape[2]
    bf16 = jnp.bfloat16
    dma = pltpu.SemaphoreType.DMA
    anywhere = pl.BlockSpec(memory_space=pl.ANY)
    return pl.pallas_call(
        functools.partial(layer_kernel, n),
        out_shape=jax.ShapeDtypeStruct(packed.shape, bf16),
        in_specs=[anywhere] * 3,
        out_specs=anywhere,
        scratch_shapes=[
            pltpu.VMEM(w_in.shape, bf16),
            pltpu.VMEM(w_out.shape, bf16),
            pltpu.VMEM((chunks, 4, block, width), bf16),
            pltpu.VMEM((4 * block, quarter), bf16),
            pltpu.VMEM((chunks, 4, block, width), bf16),
            pltpu.VMEM((chunks, 2, block, width), bf16),
            pltpu.VMEM((chunks, block, width), bf16),
            dma((chunks,)),
            dma((2,)),
            dma((chunks, n)),
            dma((chunks, n)),
            dma((9, chunks)),
            dma((9, chunks)),
            dma((3, chunks, LAST_PIECES)),
            dma((3, chunks, LAST_PIECES)),
            dma((chunks, LAST_PIECES, n)),
            dma((chunks, LAST_PIECES, n)),
            dma((chunks, LAST_PIECES)),
        ],
        compiler_params=pltpu.CompilerParams(
            collective_id=0, has_side_effects=True, vmem_limit_bytes=60 * 1024 * 1024
        ),
    )(packed, w_in, w_out)


def plain(tokens, token_ids, table, w_in, w_out):
    groups = lax.axis_size("expert")
    exp_local = w_in.shape[0]
    experts = groups * exp_local
    tok_rows, width = tokens.shape
    slots = max(2, 2 * tok_rows // experts)
    quarter = w_out.shape[1]
    chosen = jnp.take(table, token_ids, axis=0)
    expert_hot = (chosen[:, None] == jnp.arange(experts, dtype=jnp.int32)[None, :]).astype(
        jnp.int32
    )
    earlier = jnp.cumsum(expert_hot, axis=0) - expert_hot
    rank_tok = jnp.sum(earlier * expert_hot, axis=1)
    kept = rank_tok < slots
    column = (chosen // exp_local * slots + rank_tok) * exp_local + chosen % exp_local
    placer = (
        (column[:, None] == jnp.arange(experts * slots, dtype=jnp.int32)[None, :]) & kept[:, None]
    ).astype(jnp.bfloat16)
    packed = jnp.einsum("ts,td->sd", placer, tokens, preferred_element_type=jnp.float32).astype(
        jnp.bfloat16
    )
    packed = packed.reshape(groups * slots, exp_local, width)
    arrived = lax.all_to_all(packed, "expert", split_axis=0, concat_axis=0, tiled=True)
    rows = arrived.shape[0]
    hidden = jax.nn.relu(
        jnp.einsum(
            "red,edh->reh",
            arrived,
            lax.all_gather(w_in, "pair", axis=2, tiled=True),
            preferred_element_type=jnp.float32,
        )
    ).astype(jnp.bfloat16)
    total = jnp.zeros((rows, exp_local, width), jnp.float32)
    piece = lax.all_gather(w_out, "pair", axis=1, tiled=True)
    for index in range(piece.shape[1] // quarter):
        cols = lax.dynamic_slice_in_dim(hidden, index * quarter, quarter, 2)
        part = jnp.einsum(
            "reh,ehd->red",
            cols,
            piece[:, index * quarter : (index + 1) * quarter],
            preferred_element_type=jnp.float32,
        ).astype(jnp.bfloat16)
        total = total + lax.optimization_barrier(part).astype(jnp.float32)
    result = total.astype(jnp.bfloat16)
    returned = lax.all_to_all(result, "expert", split_axis=0, concat_axis=0, tiled=True)
    flat = returned.reshape(experts * slots, width)
    return jnp.dot(placer, flat, preferred_element_type=jnp.float32).astype(jnp.bfloat16)


def on_device(tokens, token_ids, table, w_in, w_out):
    n = lax.axis_size("expert")
    me = lax.axis_index("expert")
    exp_local = w_in.shape[0]
    experts = n * exp_local
    tok_rows, width = tokens.shape
    slots = max(2, 2 * tok_rows // experts)
    if slots % ROWS or table.shape[0] % LANES or lax.axis_size("pair") != 4 or experts > 256 or n < 8 or n & (n - 1):
        return plain(tokens, token_ids, table, w_in, w_out)
    per_expert = slots // ROWS

    chosen = look_up(table, token_ids)
    hot = chosen[:, None] == jnp.arange(experts, dtype=jnp.int32)[None, :]
    before = jnp.arange(tok_rows)[:, None] > jnp.arange(tok_rows)[None, :]
    earlier = exact_dot(before.astype(jnp.bfloat16), hot.astype(jnp.bfloat16))
    rank = jnp.sum(jnp.where(hot, earlier, 0.0), axis=1).astype(jnp.int32)
    ahead = jnp.bitwise_xor(chosen // exp_local, me)
    chunk = chosen % exp_local * per_expert + rank // ROWS
    column = jnp.where(rank < slots, (chunk * n + ahead) * ROWS + rank % ROWS, -1)

    places = jnp.arange(experts * slots, dtype=jnp.int32)
    placer = (places[:, None] == column[None, :]).astype(jnp.bfloat16)
    packed = exact_dot(placer, tokens).astype(jnp.bfloat16)
    packed = packed.reshape(exp_local * per_expert, n * ROWS, width)
    back = expert_layer(packed, w_in, w_out, n).reshape(experts * slots, width)
    picker = (column[:, None] == places[None, :]).astype(jnp.bfloat16)
    return exact_dot(picker, back).astype(jnp.bfloat16)


def solution(mesh):
    in_specs = (
        P(("expert", "pair"), None),
        P(("expert", "pair")),
        P(),
        P("expert", None, "pair"),
        P("expert", "pair", None),
    )
    out_specs = P(("expert", "pair"), None)
    return jax.shard_map(
        on_device, mesh=mesh, in_specs=in_specs, out_specs=out_specs, check_vma=False
    )
```

profile of v0, /device:TPU:0, one launch (start us, length us, event | category | flops | bytes accessed | tf_op | source)
XLA Modules:
  0.0 173.2 jit_solution(6394004169689579199)
XLA Ops:
  0.0 0.0 copy-start
  0.0 0.8 add_select_fusion.5
  0.8 1.1 fusion
  1.9 0.2 fusion.1
  2.1 0.0 copy-done
  2.1 3.5 %convolution_convert_fusion = bf16[768,2048]{1,0:T(8,128)(2,1)} fusion(bf16[384,2048]{1,0:T(8,128)(2,1)S(1)} %copy-done, s32[384]{0:T(512)S(1)} %fusion.14), kind=kOutput, calls=%fused_computation | convolution fusion | flops 1209827328 | bytes 4720128 | tf_op jit(solution)/shard_map/dot_general | solution.py:18
  5.6 163.1 %shard_map.55 = bf16[6,128,2048]{2,1,0:T(8,128)(2,1)} custom-call(bf16[6,128,2048]{2,1,0:T(8,128)(2,1)} %bitcast.8, bf16[2,2048,512]{2,1,0:T(8,128)(2,1)} %w_in.1, bf16[2,512,2048]{2,1,0:T(8,128)(2,1)} %w_out.1), custom_call_target="tpu_custom_call" | custom-call | tf_op jit(solution)/shard_map/pallas_call | solution.py:272
  168.7 4.5 %convolution_convert_fusion.1 = bf16[384,2048]{1,0:T(8,128)(2,1)} fusion(bf16[768,2048]{1,0:T(8,128)(2,1)} %bitcast.7, s32[384]{0:T(512)S(1)} %fusion.14), kind=kOutput, calls=%fused_computation.1 | convolution fusion | flops 1209040896 | bytes 4720128 | tf_op jit(solution)/shard_map/dot_general | solution.py:18
  (2 shorter events, 0.0 us)
Async XLA Ops:
  0.0 2.1 %copy-start = (bf16[384,2048]{1,0:T(8,128)(2,1)S(1)}, bf16[384,2048]{1,0:T(8,128)(2,1)}, u32[]{:S(2)}) copy-start(bf16[384,2048]{1,0:T(8,128)(2,1)} %param.5) | copy-start | bytes 4718596
where the time goes:
time: 174 us; the launch traced here: 173 us
  Pallas kernels  163 us (94%)
  matrix products  9.18 us (5%)
    pallas_call x1, Pallas kernels, expert_layer(): pl.pallas_call(functools.partial(layer_kernel, n), out_shape=jax.ShapeDty...  163 us
    dot_general x4, matrix products, exact_dot(): return jnp.dot(a, b, preferred_element_type=jnp.float32)  9.18 us

commit v1 on v0

v1 whole, which is shorter than its diff:
```python
import functools

import jax
import jax.numpy as jnp
from jax import lax
from jax.experimental import pallas as pl
from jax.experimental.pallas import tpu as pltpu
from jax.sharding import PartitionSpec as P

ROWS = 16
TILE = 256
LANES = 128
MESH = pl.DeviceIdType.MESH


def exact_dot(a, b):
    return jnp.dot(a, b, preferred_element_type=jnp.float32)


def across(me, j):
    other = me
    bit = 1
    while bit <= j:
        if j & bit:
            other = other + bit * (1 - 2 * (me // bit % 2))
        bit *= 2
    return other


def places(shape, dim):
    return lax.broadcasted_iota(jnp.int32, shape, dim)


def one_hot(flags):
    return jnp.where(flags, 1.0, 0.0).astype(jnp.bfloat16)


def slot_of_token(ids, table, me, exp_local, n, slots, per_expert):
    tok = ids.shape[1]
    lines = table.astype(jnp.float32).astype(jnp.bfloat16)
    line = one_hot(places((lines.shape[0], tok), 0) == ids // LANES)
    found = lax.dot_general(
        lines, line, (((0,), (0,)), ((), ())), preferred_element_type=jnp.float32
    )
    lane = places((LANES, tok), 0) == ids % LANES
    chosen = jnp.sum(jnp.where(lane, found, 0.0), axis=0, keepdims=True).astype(jnp.int32)
    hot = places((exp_local * n, tok), 0) == chosen
    before = places((tok, tok), 0) < places((tok, tok), 1)
    earlier = exact_dot(one_hot(hot), one_hot(before))
    rank = jnp.sum(jnp.where(hot, earlier, 0.0), axis=0, keepdims=True).astype(jnp.int32)
    group = chosen // exp_local
    ahead = jnp.bitwise_xor(group, me)
    chunk = chosen % exp_local * per_expert + rank // ROWS
    return jnp.where(rank < slots, (chunk * n + ahead) * ROWS + rank % ROWS, -1)


def layer_kernel(
    n,
    slots,
    ids_in,
    table_in,
    tokens_in,
    w_in,
    w_out,
    result,
    ids,
    table,
    tokens,
    packed,
    back,
    column,
    mixed,
    first,
    second,
    rows,
    hidden,
    part,
    near,
    far,
    in_sem,
    out_sem,
    go_sem,
    come_sem,
    pair_go,
    pair_come,
    part_go,
    part_come,
    ret_go,
    ret_come,
):
    chunks, block, width = packed.shape
    exp_local = w_in.shape[0]
    per_expert = chunks // exp_local
    half = n // 2
    me = lax.axis_index("expert")
    at = lax.axis_index("pair")
    core = {"pair": at + 1 - 2 * (at % 2)}
    chip = {"pair": (at + 2) % 4}
    ahead = [{"expert": across(me, j)} for j in range(n)]

    loads = [
        pltpu.make_async_copy(src, dst, in_sem.at[k])
        for k, (src, dst) in enumerate(
            [(ids_in, ids), (table_in, table), (tokens_in, tokens), (w_in, first), (w_out, second)]
        )
    ]
    for copy in loads:
        copy.start()

    barrier = pltpu.get_barrier_semaphore()
    for peer in [core, chip] + ahead[1:]:
        pl.semaphore_signal(barrier, inc=1, device_id=peer, device_id_type=MESH)

    loads[0].wait()
    loads[1].wait()
    slot = slot_of_token(ids[...].reshape(1, ids.shape[0]), table[...], me, exp_local, n, slots, per_expert)
    tok = slot.shape[1]
    column[...] = jnp.transpose(jnp.broadcast_to(slot, (LANES, tok)))
    loads[2].wait()

    def copy_to(src, dst, send, recv, peer):
        return pltpu.make_async_remote_copy(
            src_ref=src,
            dst_ref=dst,
            send_sem=send,
            recv_sem=recv,
            device_id=peer,
            device_id_type=MESH,
        )

    def blocks(lo, hi):
        return pl.ds(lo * ROWS, (hi - lo) * ROWS)

    def span(c, lo, hi):
        return pl.ds(c * block + lo * ROWS, (hi - lo) * ROWS)

    own = blocks(0, 1)
    groups = [(1, 2), (2, half), (half, n)]
    group_of = [g for j in range(n) for g in range(3) if groups[g][0] <= max(j, 1) < groups[g][1]]
    bounds = [(0, half), (half, n)]

    def send_block(c, j):
        some = blocks(j, j + 1)
        recv = come_sem.at[c, group_of[j]]
        copy_to(packed.at[c, some], rows.at[c, 0, some], go_sem, recv, ahead[j]).start()

    def wait_blocks(c, g):
        some = blocks(*groups[g])
        copy_to(
            packed.at[c, some], rows.at[c, 0, some], go_sem, come_sem.at[c, g], ahead[1]
        ).wait_recv()

    def to_pair(kind, c, h, some, start):
        if kind == 0:
            src, dst, peer = rows.at[c, 0, some], rows.at[c, 2, some], chip
        elif kind == 1:
            src, dst, peer = rows.at[c, 0, some], rows.at[c, 1, some], core
        else:
            src, dst, peer = rows.at[c, 2, some], rows.at[c, 3, some], core
        copy = copy_to(src, dst, pair_go.at[kind], pair_come.at[kind, c, h], peer)
        if start:
            copy.start()
        else:
            copy.wait_recv()

    def spread(c, h, lo, hi):
        to_pair(0, c, h, blocks(lo, hi), True)
        to_pair(1, c, h, blocks(lo, hi), True)

    def pack(c):
        placer = one_hot(places((block, tok), 0) + c * block == slot)
        wide_tile = 4 * TILE

        def step(t, carry):
            cols = pl.ds(pl.multiple_of(t * wide_tile, wide_tile), wide_tile)
            x = exact_dot(placer, tokens[:, cols]).astype(jnp.bfloat16)
            packed[c, :, cols] = x
            rows[c, 0, own, cols] = x[:ROWS]
            return carry

        lax.fori_loop(0, width // wide_tile, step, 0)

    others = list(range(half, n)) + list(range(2, half))
    pack(0)
    pack(1)
    pl.semaphore_wait(barrier, n + 1)
    for c in range(chunks):
        if c > 1:
            pack(c)
        spread(c, 0, 0, 1)
        send_block(c, 1)
        if c == 0:
            for j in others:
                send_block(c, j)
    for c in range(1, chunks):
        for j in others:
            send_block(c, j)
    for c in range(chunks):
        wait_blocks(c, 0)
        spread(c, 0, 1, 2)

    def spread_rest(c, h):
        wait_blocks(c, 1 + h)
        spread(c, h, *groups[1 + h])

    def relay(c, h):
        to_pair(0, c, h, blocks(*bounds[h]), False)
        to_pair(2, c, h, blocks(*bounds[h]), True)

    def to_part(kind, c, p, some, start):
        if kind == 0:
            src, dst, peer = part.at[c, 3, some], near.at[c, 1, some], core
        elif kind == 1:
            src, dst, peer = part.at[c, 1, some], near.at[c, 0, some], core
        else:
            src, dst, peer = part.at[c, 2, some], far.at[c, some], chip
        copy = copy_to(src, dst, part_go.at[kind], part_come.at[kind, c, p], peer)
        if start:
            copy.start()
        else:
            copy.wait_recv()

    def compute(c, h):
        e = c // per_expert
        if (c, h) == units[0]:
            for copy in loads[3:]:
                copy.wait()
        some = blocks(*bounds[h])
        size = (bounds[h][1] - bounds[h][0]) * ROWS
        to_pair(1, c, h, some, False)
        to_pair(2, c, h, some, False)

        def project_in(t, carry):
            cols = pl.ds(pl.multiple_of(t * TILE, TILE), TILE)
            x = rows[c, :, some].reshape(4 * size, width)
            hid = exact_dot(x, first[e, :, cols])
            hidden[:, cols] = jnp.maximum(hid, 0.0).astype(jnp.bfloat16)
            return carry

        lax.fori_loop(0, first.shape[2] // TILE, project_in, 0)

        def project_out(t, carry):
            tile = 2 * TILE
            cols = pl.ds(pl.multiple_of(t * tile, tile), tile)
            y = exact_dot(hidden[...], second[e, :, cols]).astype(jnp.bfloat16)
            for k in range(4):
                part[c, k, some, cols] = y[k * size : (k + 1) * size]
            return carry

        lax.fori_loop(0, width // (2 * TILE), project_out, 0)
        to_part(0, c, h, some, True)
        to_part(1, c, h, some, True)

    def over_rows(lo, hi, body):
        def step(t, carry):
            body(pl.ds(pl.multiple_of(t * ROWS, ROWS), ROWS))
            return carry

        lax.fori_loop(lo, hi, step, 0)

    def wide(x):
        return x.astype(jnp.float32)

    def pieces(c, h):
        if (c, h) == units[-1]:
            return [(2, half, 0), (0, 2, 2)]
        return [bounds[h] + (h,)]

    def cross(c, h):
        to_part(0, c, h, blocks(*bounds[h]), False)
        for lo, hi, p in pieces(c, h):

            def add(r):
                both = wide(part[c, 2, r]) + wide(near[c, 1, r])
                part[c, 2, r] = both.astype(jnp.bfloat16)

            over_rows(lo, hi, add)
            to_part(2, c, p, blocks(lo, hi), True)

    def finish(c, h):
        to_part(1, c, h, blocks(*bounds[h]), False)
        for lo, hi, p in pieces(c, h):
            to_part(2, c, p, blocks(lo, hi), False)

            def add(r):
                both = wide(part[c, 0, r]) + wide(near[c, 0, r])
                both = both + wide(far[c, r])
                part[c, 0, r] = both.astype(jnp.bfloat16)

            over_rows(lo, hi, add)
            for j in range(max(lo, 1), hi):
                copy_to(
                    part.at[c, 0, blocks(j, j + 1)],
                    back.at[span(c, j, j + 1)],
                    ret_go,
                    ret_come.at[c, h],
                    ahead[j],
                ).start()
            if lo == 0:
                back[span(c, 0, 1)] = part[c, 0, own]

    def arrived(c, h):
        lo, hi = bounds[h]
        lo = max(lo, 1)
        copy_to(
            part.at[c, 0, blocks(lo, hi)],
            back.at[span(c, lo, hi)],
            ret_go,
            ret_come.at[c, h],
            ahead[1],
        ).wait_recv()

    def pick(ranges, more, store):
        picker = jnp.concatenate(
            [
                one_hot(column[:, : hi - lo] == places((tok, hi - lo), 1) + lo)
                for lo, hi in ranges
            ],
            axis=1,
        )

        tile = (2 if store else 4) * TILE

        def step(t, carry):
            some = pl.ds(pl.multiple_of(t * tile, tile), tile)
            x = jnp.concatenate([back[lo:hi, some] for lo, hi in ranges], axis=0)
            y = exact_dot(picker, x)
            if more:
                y = y + wide(mixed[:, some])
            mixed[:, some] = y.astype(jnp.bfloat16)
            return carry

        if store:
            for t in range(width // tile):
                step(t, 0)
                cols = pl.ds(t * tile, tile)
                copy = pltpu.make_async_copy(
                    mixed.at[:, cols], result.at[:, cols], out_sem.at[t]
                )
                copy.start()
                stores.append(copy)
        else:
            lax.fori_loop(0, width // tile, step, 0)

    units = unit_order(chunks)
    count = len(units)
    for i in range(count + 1):
        if i < count:
            spread_rest(*units[i])
        if i >= 1:
            relay(*units[i - 1])
            compute(*units[i - 1])
            cross(*units[i - 1])
        if i >= 2:
            finish(*units[i - 2])

    def slots_of(lo, hi):
        return [(c * block, (c + 1) * block) for c in range(lo, hi)]

    stores = []
    early = chunks // 2
    last = chunks - 1
    for c in range(early):
        arrived(c, 0)
        arrived(c, 1)
    pick(slots_of(0, early), False, False)
    arrived(early, 0)
    arrived(early, 1)
    finish(*units[-1])
    pick(slots_of(early, early + 1), True, False)
    for c in range(early + 1, last):
        arrived(c, 0)
        arrived(c, 1)
    arrived(last, 1)
    pick(slots_of(early + 1, last) + [(last * block + half * ROWS, chunks * block)], True, False)
    arrived(last, 0)
    pick([(last * block, last * block + half * ROWS)], True, True)

    every = rows.at[:, 0]
    but_own = pl.ds(ROWS, block - ROWS)
    copy_to(packed.at[:, but_own], rows.at[:, 0, but_own], go_sem, go_sem, core).wait_send()
    for kind in range(3):
        copy_to(every, every, pair_go.at[kind], go_sem, core).wait_send()
        copy_to(every, every, part_go.at[kind], go_sem, core).wait_send()
    copy_to(part.at[:, 0, but_own], rows.at[:, 0, but_own], ret_go, go_sem, core).wait_send()
    for copy in stores:
        copy.wait()


def unit_order(chunks):
    early = chunks // 2
    order = [(c, h) for c in range(early) for h in (1, 0)]
    order += [(c, 1) for c in range(early, chunks)]
    return order + [(c, 0) for c in range(early, chunks)]


def expert_layer(ids, table, tokens, w_in, w_out, n, slots):
    exp_local, width, quarter = w_in.shape
    tok = tokens.shape[0]
    chunks = exp_local * slots // ROWS
    block = n * ROWS
    bf16 = jnp.bfloat16
    dma = pltpu.SemaphoreType.DMA
    anywhere = pl.BlockSpec(memory_space=pl.ANY)
    return pl.pallas_call(
        functools.partial(layer_kernel, n, slots),
        out_shape=jax.ShapeDtypeStruct(tokens.shape, bf16),
        in_specs=[anywhere] * 5,
        out_specs=anywhere,
        scratch_shapes=[
            pltpu.VMEM(ids.shape, jnp.int32),
            pltpu.VMEM(table.shape, jnp.int32),
            pltpu.VMEM(tokens.shape, bf16),
            pltpu.VMEM((chunks, block, width), bf16),
            pltpu.VMEM((chunks * block, width), bf16),
            pltpu.VMEM((tok, LANES), jnp.int32),
            pltpu.VMEM(tokens.shape, bf16),
            pltpu.VMEM(w_in.shape, bf16),
            pltpu.VMEM(w_out.shape, bf16),
            pltpu.VMEM((chunks, 4, block, width), bf16),
            pltpu.VMEM((2 * block, quarter), bf16),
            pltpu.VMEM((chunks, 4, block, width), bf16),
            pltpu.VMEM((chunks, 2, block, width), bf16),
            pltpu.VMEM((chunks, block, width), bf16),
            dma((5,)),
            dma((width // TILE,)),
            dma,
            dma((chunks, 3)),
            dma((3,)),
            dma((3, chunks, 2)),
            dma((3,)),
            dma((3, chunks, 3)),
            dma,
            dma((chunks, 2)),
        ],
        compiler_params=pltpu.CompilerParams(
            collective_id=0, has_side_effects=True, vmem_limit_bytes=62 * 1024 * 1024
        ),
    )(ids, table, tokens, w_in, w_out)


def plain(tokens, token_ids, table, w_in, w_out):
    groups = lax.axis_size("expert")
    exp_local = w_in.shape[0]
    experts = groups * exp_local
    tok_rows, width = tokens.shape
    slots = max(2, 2 * tok_rows // experts)
    quarter = w_out.shape[1]
    chosen = jnp.take(table, token_ids, axis=0)
    expert_hot = (chosen[:, None] == jnp.arange(experts, dtype=jnp.int32)[None, :]).astype(
        jnp.int32
    )
    earlier = jnp.cumsum(expert_hot, axis=0) - expert_hot
    rank_tok = jnp.sum(earlier * expert_hot, axis=1)
    kept = rank_tok < slots
    column = (chosen // exp_local * slots + rank_tok) * exp_local + chosen % exp_local
    placer = (
        (column[:, None] == jnp.arange(experts * slots, dtype=jnp.int32)[None, :]) & kept[:, None]
    ).astype(jnp.bfloat16)
    packed = jnp.einsum("ts,td->sd", placer, tokens, preferred_element_type=jnp.float32).astype(
        jnp.bfloat16
    )
    packed = packed.reshape(groups * slots, exp_local, width)
    arrived = lax.all_to_all(packed, "expert", split_axis=0, concat_axis=0, tiled=True)
    rows = arrived.shape[0]
    hidden = jax.nn.relu(
        jnp.einsum(
            "red,edh->reh",
            arrived,
            lax.all_gather(w_in, "pair", axis=2, tiled=True),
            preferred_element_type=jnp.float32,
        )
    ).astype(jnp.bfloat16)
    total = jnp.zeros((rows, exp_local, width), jnp.float32)
    piece = lax.all_gather(w_out, "pair", axis=1, tiled=True)
    for index in range(piece.shape[1] // quarter):
        cols = lax.dynamic_slice_in_dim(hidden, index * quarter, quarter, 2)
        part = jnp.einsum(
            "reh,ehd->red",
            cols,
            piece[:, index * quarter : (index + 1) * quarter],
            preferred_element_type=jnp.float32,
        ).astype(jnp.bfloat16)
        total = total + lax.optimization_barrier(part).astype(jnp.float32)
    result = total.astype(jnp.bfloat16)
    returned = lax.all_to_all(result, "expert", split_axis=0, concat_axis=0, tiled=True)
    flat = returned.reshape(experts * slots, width)
    return jnp.dot(placer, flat, preferred_element_type=jnp.float32).astype(jnp.bfloat16)


def on_device(tokens, token_ids, table, w_in, w_out):
    n = lax.axis_size("expert")
    exp_local = w_in.shape[0]
    experts = n * exp_local
    tok_rows, width = tokens.shape
    slots = max(2, 2 * tok_rows // experts)
    fits = slots % ROWS == 0 and tok_rows % LANES == 0 and table.shape[0] % LANES == 0
    fits = fits and lax.axis_size("pair") == 4 and experts <= 256 and n == LANES // ROWS
    fits = fits and width % (4 * TILE) == 0 and w_in.shape[2] % TILE == 0
    if not fits or exp_local * slots // ROWS < 3:
        return plain(tokens, token_ids, table, w_in, w_out)
    return expert_layer(
        token_ids, table.reshape(-1, LANES), tokens, w_in, w_out, n, slots
    )


def solution(mesh):
    in_specs = (
        P(("expert", "pair"), None),
        P(("expert", "pair")),
        P(),
        P("expert", None, "pair"),
        P("expert", "pair", None),
    )
    out_specs = P(("expert", "pair"), None)
    return jax.shard_map(
        on_device, mesh=mesh, in_specs=in_specs, out_specs=out_specs, check_vma=False
    )
```

time: 174 us -> 158 us (0.908)
  matrix products: 9.18 us -> 0 us
  Pallas kernels: 163 us -> 155 us
  local copies, waits for them, and re-layouts: 0.01 us -> 2.73 us
    dot_general x4 -> x0, matrix products: 9.18 us -> none  [exact_dot(): return jnp.dot(a, b, preferred_element_type=jnp.float32)]
    pallas_call x1, Pallas kernels: 163 us -> 155 us  [expert_layer(): pl.pallas_call(functools.partial(layer_kernel, n, slots), out_shape=jax.S...]
    unnamed x2 -> x1, local copies, waits for them, and re-layouts: 0.01 us -> 2.73 us
where the time goes in v1:
time: 158 us
  Pallas kernels  155 us (98%)
  local copies, waits for them, and re-layouts  2.73 us (2%)
    pallas_call x1, Pallas kernels, expert_layer(): pl.pallas_call(functools.partial(layer_kernel, n, slots), out_shape=jax.S...  155 us

profile of v1, /device:TPU:0, one launch (start us, length us, event | category | flops | bytes accessed | tf_op | source)
XLA Modules:
  0.0 158.2 jit_solution(605913470190424368)
XLA Ops:
  0.0 155.4 %shard_map.55 = bf16[384,2048]{1,0:T(8,128)(2,1)} custom-call(s32[384]{0:T(512)} %ids_in.1, s32[64,128]{1,0:T(8,128)} %bitcast.1, bf16[384,2048]{1,0:T(8,128)(2,1)} %tokens_in.1, bf16[2,2048,512]{2,1,0:T(8,128)(2,1)} %w_in.1, bf16[2,512,2048]{2,1,0:T(8,128)(2,1)} %w_out.1), custom_call_target="tpu_custom_call" | custom-call | tf_op jit(solution)/shard_map/pallas_call | solution.py:405
  155.4 2.7 %copy.7 = bf16[384,2048]{1,0:T(8,128)(2,1)} copy(bf16[384,2048]{1,0:T(8,128)(2,1)} %shard_map.55) | data formatting | bytes 3145728

commit v2 on v1

--- a/solution.py
+++ b/solution.py
@@ -180,7 +180,12 @@
 
         lax.fori_loop(0, width // wide_tile, step, 0)
 
-    others = list(range(half, n)) + list(range(2, half))
+    early, steps, spreads = plan(chunks)
+
+    def dispatch(c, h):
+        for j in range(*groups[1 + h]):
+            send_block(c, j)
+
     pack(0)
     pack(1)
     pl.semaphore_wait(barrier, n + 1)
@@ -189,19 +194,18 @@
             pack(c)
         spread(c, 0, 0, 1)
         send_block(c, 1)
+        dispatch(c, 0)
         if c == 0:
-            for j in others:
-                send_block(c, j)
+            dispatch(0, 1)
     for c in range(1, chunks):
-        for j in others:
-            send_block(c, j)
-    for c in range(chunks):
-        wait_blocks(c, 0)
-        spread(c, 0, 1, 2)
-
+        dispatch(c, 1)
     def spread_rest(c, h):
         wait_blocks(c, 1 + h)
         spread(c, h, *groups[1 + h])
+
+    def spread_beside(c):
+        wait_blocks(c, 0)
+        spread(c, 0, 1, 2)
 
     def relay(c, h):
         to_pair(0, c, h, blocks(*bounds[h]), False)
@@ -222,7 +226,7 @@
 
     def compute(c, h):
         e = c // per_expert
-        if (c, h) == units[0]:
+        if (c, h) == steps[0]:
             for copy in loads[3:]:
                 copy.wait()
         some = blocks(*bounds[h])
@@ -262,8 +266,8 @@
         return x.astype(jnp.float32)
 
     def pieces(c, h):
-        if (c, h) == units[-1]:
-            return [(2, half, 0), (0, 2, 2)]
+        if (c, h) == steps[-1]:
+            return [(2, half, 0), (1, 2, 2), (0, 1, 3)]
         return [bounds[h] + (h,)]
 
     def cross(c, h):
@@ -327,38 +331,34 @@
             y = exact_dot(picker, x)
             if more:
                 y = y + wide(mixed[:, some])
-            mixed[:, some] = y.astype(jnp.bfloat16)
+            (result if store else mixed)[:, some] = y.astype(jnp.bfloat16)
             return carry
 
         if store:
             for t in range(width // tile):
                 step(t, 0)
-                cols = pl.ds(t * tile, tile)
-                copy = pltpu.make_async_copy(
-                    mixed.at[:, cols], result.at[:, cols], out_sem.at[t]
-                )
-                copy.start()
-                stores.append(copy)
         else:
             lax.fori_loop(0, width // tile, step, 0)
 
-    units = unit_order(chunks)
-    count = len(units)
-    for i in range(count + 1):
-        if i < count:
-            spread_rest(*units[i])
-        if i >= 1:
-            relay(*units[i - 1])
-            compute(*units[i - 1])
-            cross(*units[i - 1])
-        if i >= 2:
-            finish(*units[i - 2])
+    for c in range(early):
+        spread_beside(c)
+        spread_rest(c, 0)
+    for i, (c, h) in enumerate(steps):
+        relay(c, h)
+        compute(c, h)
+        cross(c, h)
+        if i == 0:
+            for late in range(early, chunks):
+                spread_beside(late)
+        else:
+            finish(*steps[i - 1])
+        if spreads[i]:
+            spread_rest(*spreads[i])
 
     def slots_of(lo, hi):
         return [(c * block, (c + 1) * block) for c in range(lo, hi)]
 
     stores = []
-    early = chunks // 2
     last = chunks - 1
     for c in range(early):
         arrived(c, 0)
@@ -366,16 +366,13 @@
     pick(slots_of(0, early), False, False)
     arrived(early, 0)
     arrived(early, 1)
-    finish(*units[-1])
+    finish(*steps[-1])
     pick(slots_of(early, early + 1), True, False)
     for c in range(early + 1, last):
         arrived(c, 0)
         arrived(c, 1)
     arrived(last, 1)
     pick(slots_of(early + 1, last) + [(last * block + half * ROWS, chunks * block)], True, False)
-    arrived(last, 0)
-    pick([(last * block, last * block + half * ROWS)], True, True)
-
     every = rows.at[:, 0]
     but_own = pl.ds(ROWS, block - ROWS)
     copy_to(packed.at[:, but_own], rows.at[:, 0, but_own], go_sem, go_sem, core).wait_send()
@@ -383,15 +380,23 @@
         copy_to(every, every, pair_go.at[kind], go_sem, core).wait_send()
         copy_to(every, every, part_go.at[kind], go_sem, core).wait_send()
     copy_to(part.at[:, 0, but_own], rows.at[:, 0, but_own], ret_go, go_sem, core).wait_send()
-    for copy in stores:
-        copy.wait()
-
-
-def unit_order(chunks):
+    arrived(last, 0)
+    pick([(last * block, last * block + half * ROWS)], True, True)
+
+
+def plan(chunks):
     early = chunks // 2
-    order = [(c, h) for c in range(early) for h in (1, 0)]
-    order += [(c, 1) for c in range(early, chunks)]
-    return order + [(c, 0) for c in range(early, chunks)]
+    steps = [(0, 0)]
+    for c in range(1, early):
+        steps += [(c, 0), (c - 1, 1)]
+    steps += [(c, 1) for c in range(early - 1, chunks)]
+    steps += [(c, 0) for c in range(early, chunks)]
+    spreads = [(c, 1) for c in range(chunks)] + [(c, 0) for c in range(early, chunks)]
+    ahead = []
+    for c, h in steps:
+        wanted = h == 1 or not 2 <= c < early
+        ahead.append(spreads.pop(0) if spreads and wanted else None)
+    return early, steps, ahead
 
 
 def expert_layer(ids, table, tokens, w_in, w_out, n, slots):
@@ -404,9 +409,9 @@
     anywhere = pl.BlockSpec(memory_space=pl.ANY)
     return pl.pallas_call(
         functools.partial(layer_kernel, n, slots),
-        out_shape=jax.ShapeDtypeStruct(tokens.shape, bf16),
+        out_shape=pltpu.VMEM(tokens.shape, bf16),
         in_specs=[anywhere] * 5,
-        out_specs=anywhere,
+        out_specs=pl.BlockSpec(memory_space=pltpu.VMEM),
         scratch_shapes=[
             pltpu.VMEM(ids.shape, jnp.int32),
             pltpu.VMEM(table.shape, jnp.int32),
@@ -429,12 +434,12 @@
             dma((3,)),
             dma((3, chunks, 2)),
             dma((3,)),
-            dma((3, chunks, 3)),
+            dma((3, chunks, 4)),
             dma,
             dma((chunks, 2)),
         ],
         compiler_params=pltpu.CompilerParams(
-            collective_id=0, has_side_effects=True, vmem_limit_bytes=62 * 1024 * 1024
+            collective_id=0, has_side_effects=True, vmem_limit_bytes=60 * 1024 * 1024
         ),
     )(ids, table, tokens, w_in, w_out)
 

time: 158 us -> 152 us (0.962)
  Pallas kernels: 155 us -> 150 us
  local copies, waits for them, and re-layouts: 2.73 us -> 1.15 us
    pallas_call x1, Pallas kernels: 155 us -> 150 us  [expert_layer(): pl.pallas_call(functools.partial(layer_kernel, n, slots), out_shape=pltpu...]
    unnamed x1, local copies, waits for them, and re-layouts: 2.73 us -> 1.15 us
where the time goes in v2:
time: 152 us
  Pallas kernels  150 us (99%)
    pallas_call x1, Pallas kernels, expert_layer(): pl.pallas_call(functools.partial(layer_kernel, n, slots), out_shape=pltpu...  150 us

profile of v2, /device:TPU:0, one launch (start us, length us, event | category | flops | bytes accessed | tf_op | source)
XLA Modules:
  0.0 151.6 jit_solution(10248548453253202258)
XLA Ops:
  0.0 150.5 %shard_map.55 = bf16[384,2048]{1,0:T(8,128)(2,1)S(1)} custom-call(s32[384]{0:T(512)} %ids_in.1, s32[64,128]{1,0:T(8,128)} %bitcast.1, bf16[384,2048]{1,0:T(8,128)(2,1)} %tokens_in.1, bf16[2,2048,512]{2,1,0:T(8,128)(2,1)} %w_in.1, bf16[2,512,2048]{2,1,0:T(8,128)(2,1)} %w_out.1), custom_call_target="tpu_custom_call" | custom-call | tf_op jit(solution)/shard_map/pallas_call | solution.py:410
  150.5 1.1 copy.7

commit v3 on v2

--- a/solution.py
+++ b/solution.py
@@ -78,13 +78,13 @@
     near,
     far,
     in_sem,
-    out_sem,
     go_sem,
     come_sem,
     pair_go,
     pair_come,
     part_go,
     part_come,
+    far_come,
     ret_go,
     ret_come,
 ):
@@ -218,7 +218,8 @@
             src, dst, peer = part.at[c, 1, some], near.at[c, 0, some], core
         else:
             src, dst, peer = part.at[c, 2, some], far.at[c, some], chip
-        copy = copy_to(src, dst, part_go.at[kind], part_come.at[kind, c, p], peer)
+        recv = far_come.at[c, p] if kind == 2 else part_come.at[kind, c, p]
+        copy = copy_to(src, dst, part_go.at[kind], recv, peer)
         if start:
             copy.start()
         else:
@@ -266,20 +267,33 @@
         return x.astype(jnp.float32)
 
     def pieces(c, h):
-        if (c, h) == steps[-1]:
-            return [(2, half, 0), (1, 2, 2), (0, 1, 3)]
+        if h == 0 and c >= early:
+            return [(2, half, 0), (1, 2, 2)]
         return [bounds[h] + (h,)]
 
     def cross(c, h):
         to_part(0, c, h, blocks(*bounds[h]), False)
+
+        def add(r):
+            both = wide(part[c, 2, r]) + wide(near[c, 1, r])
+            part[c, 2, r] = both.astype(jnp.bfloat16)
+
         for lo, hi, p in pieces(c, h):
-
-            def add(r):
-                both = wide(part[c, 2, r]) + wide(near[c, 1, r])
-                part[c, 2, r] = both.astype(jnp.bfloat16)
-
             over_rows(lo, hi, add)
             to_part(2, c, p, blocks(lo, hi), True)
+
+    def cross_own(c):
+        both = wide(part[c, 2, own]) + wide(near[c, 1, own])
+        part[c, 2, own] = both.astype(jnp.bfloat16)
+        to_part(2, c, 3, own, True)
+
+    def sum_up(c, r):
+        both = wide(part[c, 0, r]) + wide(near[c, 0, r])
+        return (both + wide(far[c, r])).astype(jnp.bfloat16)
+
+    def finish_own(c):
+        to_part(2, c, 3, own, False)
+        back[span(c, 0, 1)] = sum_up(c, own)
 
     def finish(c, h):
         to_part(1, c, h, blocks(*bounds[h]), False)
@@ -287,9 +301,7 @@
             to_part(2, c, p, blocks(lo, hi), False)
 
             def add(r):
-                both = wide(part[c, 0, r]) + wide(near[c, 0, r])
-                both = both + wide(far[c, r])
-                part[c, 0, r] = both.astype(jnp.bfloat16)
+                part[c, 0, r] = sum_up(c, r)
 
             over_rows(lo, hi, add)
             for j in range(max(lo, 1), hi):
@@ -340,39 +352,50 @@
         else:
             lax.fori_loop(0, width // tile, step, 0)
 
-    for c in range(early):
+    first_beside = min(early + 1, chunks)
+    spread_beside(0)
+    spread_rest(0, 0)
+    for c in range(1, first_beside):
         spread_beside(c)
+    for c in range(1, min(2, early)):
         spread_rest(c, 0)
     for i, (c, h) in enumerate(steps):
         relay(c, h)
         compute(c, h)
         cross(c, h)
         if i == 0:
-            for late in range(early, chunks):
+            for late in range(first_beside, chunks):
                 spread_beside(late)
+            for late in range(2, early):
+                spread_rest(late, 0)
         else:
             finish(*steps[i - 1])
-        if spreads[i]:
-            spread_rest(*spreads[i])
+        for unit in spreads[i]:
+            spread_rest(*unit)
 
     def slots_of(lo, hi):
         return [(c * block, (c + 1) * block) for c in range(lo, hi)]
 
-    stores = []
     last = chunks - 1
+    for c in range(early, chunks):
+        cross_own(c)
     for c in range(early):
         arrived(c, 0)
         arrived(c, 1)
     pick(slots_of(0, early), False, False)
-    arrived(early, 0)
-    arrived(early, 1)
     finish(*steps[-1])
-    pick(slots_of(early, early + 1), True, False)
-    for c in range(early + 1, last):
+
+    def others_of(lo, hi):
+        return [(c * block + ROWS, (c + 1) * block) for c in range(lo, hi)]
+
+    for c in range(early, last - 1):
         arrived(c, 0)
         arrived(c, 1)
-    arrived(last, 1)
-    pick(slots_of(early + 1, last) + [(last * block + half * ROWS, chunks * block)], True, False)
+    pick(others_of(early, last - 1), True, False)
+    arrived(last - 1, 0)
+    arrived(last - 1, 1)
+    pick(others_of(last - 1, last), True, False)
+
     every = rows.at[:, 0]
     but_own = pl.ds(ROWS, block - ROWS)
     copy_to(packed.at[:, but_own], rows.at[:, 0, but_own], go_sem, go_sem, core).wait_send()
@@ -381,21 +404,31 @@
         copy_to(every, every, part_go.at[kind], go_sem, core).wait_send()
     copy_to(part.at[:, 0, but_own], rows.at[:, 0, but_own], ret_go, go_sem, core).wait_send()
     arrived(last, 0)
-    pick([(last * block, last * block + half * ROWS)], True, True)
+    arrived(last, 1)
+    for c in range(early, chunks):
+        finish_own(c)
+    own_slots = [(c * block, c * block + ROWS) for c in range(early, last)]
+    pick(own_slots + slots_of(last, chunks), True, True)
 
 
 def plan(chunks):
     early = chunks // 2
-    steps = [(0, 0)]
-    for c in range(1, early):
-        steps += [(c, 0), (c - 1, 1)]
+    steps = [(c, 0) for c in range(early - 1)]
+    steps += [(c, 1) for c in range(early - 1)] + [(early - 1, 0)]
     steps += [(c, 1) for c in range(early - 1, chunks)]
     steps += [(c, 0) for c in range(early, chunks)]
-    spreads = [(c, 1) for c in range(chunks)] + [(c, 0) for c in range(early, chunks)]
+    waiting = [(c, h) for c, h in steps if h == 1 or c >= early]
     ahead = []
-    for c, h in steps:
-        wanted = h == 1 or not 2 <= c < early
-        ahead.append(spreads.pop(0) if spreads and wanted else None)
+    done = 0
+    for i in range(len(steps)):
+        later = [u for u in steps[i + 1 :] if u in waiting]
+        depth = 1 if i in (0, early - 1, early) else 2
+        if steps[i] in [(chunks - 2, 1), (chunks - 1, 1)]:
+            depth = 3
+        wanted = later[:depth]
+        upto = max([done] + [waiting.index(u) + 1 for u in wanted])
+        ahead.append(waiting[done:upto])
+        done = upto
     return early, steps, ahead
 
 
@@ -428,13 +461,13 @@
             pltpu.VMEM((chunks, 2, block, width), bf16),
             pltpu.VMEM((chunks, block, width), bf16),
             dma((5,)),
-            dma((width // TILE,)),
             dma,
             dma((chunks, 3)),
             dma((3,)),
             dma((3, chunks, 2)),
             dma((3,)),
-            dma((3, chunks, 4)),
+            dma((2, chunks, 2)),
+            dma((chunks, 4)),
             dma,
             dma((chunks, 2)),
         ],
@@ -502,7 +535,7 @@
     fits = slots % ROWS == 0 and tok_rows % LANES == 0 and table.shape[0] % LANES == 0
     fits = fits and lax.axis_size("pair") == 4 and experts <= 256 and n == LANES // ROWS
     fits = fits and width % (4 * TILE) == 0 and w_in.shape[2] % TILE == 0
-    if not fits or exp_local * slots // ROWS < 3:
+    if not fits or exp_local * slots // ROWS < 4:
         return plain(tokens, token_ids, table, w_in, w_out)
     return expert_layer(
         token_ids, table.reshape(-1, LANES), tokens, w_in, w_out, n, slots

time: 152 us -> 150 us (0.987)
  Pallas kernels: 150 us -> 148 us
    pallas_call x1, Pallas kernels: 150 us -> 148 us  [expert_layer(): pl.pallas_call(functools.partial(layer_kernel, n, slots), out_shape=pltpu...]
where the time goes in v3:
time: 150 us
  Pallas kernels  148 us (99%)
    pallas_call x1, Pallas kernels, expert_layer(): pl.pallas_call(functools.partial(layer_kernel, n, slots), out_shape=pltpu...  148 us

profile of v3, /device:TPU:0, one launch (start us, length us, event | category | flops | bytes accessed | tf_op | source)
XLA Modules:
  0.0 149.6 jit_solution(11739174566453114347)
XLA Ops:
  0.0 148.5 %shard_map.55 = bf16[384,2048]{1,0:T(8,128)(2,1)S(1)} custom-call(s32[384]{0:T(512)} %ids_in.1, s32[64,128]{1,0:T(8,128)} %bitcast.1, bf16[384,2048]{1,0:T(8,128)(2,1)} %tokens_in.1, bf16[2,2048,512]{2,1,0:T(8,128)(2,1)} %w_in.1, bf16[2,512,2048]{2,1,0:T(8,128)(2,1)} %w_out.1), custom_call_target="tpu_custom_call" | custom-call | tf_op jit(solution)/shard_map/pallas_call | solution.py:443
  148.5 1.1 copy.7

commit v4 on v3

--- a/solution.py
+++ b/solution.py
@@ -104,12 +104,11 @@
             [(ids_in, ids), (table_in, table), (tokens_in, tokens), (w_in, first), (w_out, second)]
         )
     ]
-    for copy in loads:
-        copy.start()
-
     barrier = pltpu.get_barrier_semaphore()
     for peer in [core, chip] + ahead[1:]:
         pl.semaphore_signal(barrier, inc=1, device_id=peer, device_id_type=MESH)
+    for copy in loads:
+        copy.start()
 
     loads[0].wait()
     loads[1].wait()
@@ -157,7 +156,7 @@
             src, dst, peer = rows.at[c, 0, some], rows.at[c, 1, some], core
         else:
             src, dst, peer = rows.at[c, 2, some], rows.at[c, 3, some], core
-        copy = copy_to(src, dst, pair_go.at[kind], pair_come.at[kind, c, h], peer)
+        copy = copy_to(src, dst, pair_go.at[kind], pair_come.at[min(kind, 1), c, h], peer)
         if start:
             copy.start()
         else:
@@ -232,8 +231,8 @@
                 copy.wait()
         some = blocks(*bounds[h])
         size = (bounds[h][1] - bounds[h][0]) * ROWS
-        to_pair(1, c, h, some, False)
-        to_pair(2, c, h, some, False)
+        both = rows.at[c, pl.ds(0, 2), some]
+        copy_to(both, both, pair_go.at[1], pair_come.at[1, c, h], core).wait_recv()
 
         def project_in(t, carry):
             cols = pl.ds(pl.multiple_of(t * TILE, TILE), TILE)
@@ -242,7 +241,7 @@
             hidden[:, cols] = jnp.maximum(hid, 0.0).astype(jnp.bfloat16)
             return carry
 
-        lax.fori_loop(0, first.shape[2] // TILE, project_in, 0)
+        lax.fori_loop(0, first.shape[2] // TILE, project_in, 0, unroll=True)
 
         def project_out(t, carry):
             tile = 2 * TILE
@@ -252,7 +251,7 @@
                 part[c, k, some, cols] = y[k * size : (k + 1) * size]
             return carry
 
-        lax.fori_loop(0, width // (2 * TILE), project_out, 0)
+        lax.fori_loop(0, width // (2 * TILE), project_out, 0, unroll=2)
         to_part(0, c, h, some, True)
         to_part(1, c, h, some, True)
 
@@ -464,7 +463,7 @@
             dma,
             dma((chunks, 3)),
             dma((3,)),
-            dma((3, chunks, 2)),
+            dma((2, chunks, 2)),
             dma((3,)),
             dma((2, chunks, 2)),
             dma((chunks, 4)),

time: 150 us -> 149 us (level)
  no operation moved by 1% of the time
where the time goes in v4:
time: 149 us
  Pallas kernels  147 us (99%)
    pallas_call x1, Pallas kernels, expert_layer(): pl.pallas_call(functools.partial(layer_kernel, n, slots), out_shape=pltpu...  147 us

profile of v4, /device:TPU:0, one launch (start us, length us, event | category | flops | bytes accessed | tf_op | source)
XLA Modules:
  0.0 148.6 jit_solution(18035591048295259215)
XLA Ops:
  0.0 147.4 %shard_map.55 = bf16[384,2048]{1,0:T(8,128)(2,1)S(1)} custom-call(s32[384]{0:T(512)} %ids_in.1, s32[64,128]{1,0:T(8,128)} %bitcast.1, bf16[384,2048]{1,0:T(8,128)(2,1)} %tokens_in.1, bf16[2,2048,512]{2,1,0:T(8,128)(2,1)} %w_in.1, bf16[2,512,2048]{2,1,0:T(8,128)(2,1)} %w_out.1), custom_call_target="tpu_custom_call" | custom-call | tf_op jit(solution)/shard_map/pallas_call | solution.py:442
  147.4 1.1 copy.7
